TPU v7x, 32 devices: a whole 2x2x4 slice. The times are simulated.
32 devices in a mesh: mem: 8 (over z, x), rep: 4 (over y, core).
Axes of the slice: x: 2, y: 2, z: 4, core: 2. Of those that a mesh axis runs over, the one named last changes fastest.
Arguments:
- memory: float32 [8192, 172], P('mem'), may hold values from -6 to 6
- node_slot: int32 [8192], replicated, may hold values from 0 to 8191, as said below
- event_nodes: int32 [2, 4096, 33], P(None, ('mem', 'rep')), may hold values from 0 to 8191, as said below
- event_times: int32 [2, 4096], P(None, ('mem', 'rep')), may hold values from 0 to 999
- valid_mask: int32 [2, 4096], P(None, ('mem', 'rep')), may hold values 0 or 1
- time_freq: float32 [100], replicated, may hold values from 0.001 to 1
- time_phase: float32 [100], replicated, may hold values from -3.140625 to 3.140625
- gru_input: bfloat16 [444, 516], replicated, may hold values from -0.25 to 0.25
- gru_hidden: bfloat16 [172, 516], replicated, may hold values from -0.4375 to 0.4375
- gru_in_bias: float32 [516], replicated, may hold values from -3 to 3
- gru_hid_bias: float32 [516], replicated, may hold values from -3 to 3
- w_self: float32 [172, 100], replicated, may hold values from -0.4375 to 0.4375
- w_nbr: float32 [172, 100], replicated, may hold values from -0.4375 to 0.4375
- b_embed: float32 [100], replicated, may hold values from -3 to 3
- w_dec1: float32 [200, 100], replicated, may hold values from -0.4375 to 0.4375
- b_dec1: float32 [100], replicated, may hold values from -3 to 3
- w_dec2: float32 [100], replicated, may hold values from -0.625 to 0.625
- b_dec2: float32 [1], replicated, may hold values from -3 to 3
Outputs:
- memory_out: float32 [8192, 172], P('mem')
- batch_losses: float32 [2], replicated
- w_self_out: float32 [172, 100], replicated
- w_nbr_out: float32 [172, 100], replicated
- b_embed_out: float32 [100], replicated
- w_dec1_out: float32 [200, 100], replicated
- b_dec1_out: float32 [100], replicated
- w_dec2_out: float32 [100], replicated
- b_dec2_out: float32 [1], replicated
Inputs may be any that keep to these rules, and one draw needn't show every extreme that they name: A permutation: node n's memory is row node_slot[n] of memory. `event_nodes`: columns 0, 1, 2 of an event are its source, destination and negative node; column 3 + r * 10 + k is neighbour k of column r. Among one device's events of one batch, the nodes of columns 0 and 1 whose slots lie in one block of 1024 slots are at most 64, and those of the other columns at most 620; in every such group of events one block of slots receives exactly 64 and 620.
All inputs are finite; a program needn't handle non-finite values. No bound on the sum of `valid_mask` on one device may be relied on, other than what follows from the above.
Results may differ from a plain program's by a relative error of at most 0.002.
Values may be sent and summed in bfloat16 or wider, within the bound.
A program may use at most 128 MiB of HBM per device.

v0:
```python
import jax
import jax.numpy as jnp
from jax import lax
from jax.sharding import PartitionSpec as P

step_size = 4.0


def block_loss(current, own_rows, beside_sum, neighbours, valid_part):
    w_self, w_nbr, b_embed, w_dec1, b_dec1, w_dec2, b_dec2 = current
    num_events = own_rows.shape[0] // 3
    direct = jnp.dot(own_rows, w_self.astype(jnp.bfloat16), preferred_element_type=jnp.float32)
    spread = jnp.dot(
        beside_sum, w_nbr.astype(jnp.bfloat16).astype(jnp.float32), precision=lax.Precision.HIGHEST
    )
    hidden = jnp.tanh(direct + spread * (1.0 / neighbours) + b_embed).astype(jnp.bfloat16)
    first = hidden[:num_events]
    paired = jnp.concatenate([jnp.concatenate([first, first], 0), hidden[num_events:]], 1)
    inner_act = jax.nn.relu(
        jnp.dot(paired, w_dec1.astype(jnp.bfloat16), preferred_element_type=jnp.float32) + b_dec1
    )
    logits = jnp.sum(inner_act * w_dec2, 1) + b_dec2[0]
    weights = valid_part.astype(jnp.float32)
    sign_flip = jnp.concatenate(
        [-jnp.ones((num_events,), jnp.float32), jnp.ones((num_events,), jnp.float32)]
    )
    return jnp.sum(jax.nn.softplus(sign_flip * logits) * jnp.concatenate([weights, weights]))


def normalized_step(params, gradients):
    total = jnp.zeros((), jnp.float32)
    for grad_part in gradients:
        total = total + jnp.sum(grad_part * grad_part)
    factor = step_size / (jnp.sqrt(total) + 1e-06)
    return tuple((value - factor * grad_part for value, grad_part in zip(params, gradients)))


def memory_update(mean_rest, state_bf, old_state, gru_input, gru_hidden, gru_in_bias, gru_hid_bias):
    row_width = old_state.shape[1]
    from_input = (
        jnp.dot(state_bf, gru_input[:row_width], preferred_element_type=jnp.float32)
        + jnp.dot(mean_rest, gru_input[row_width:], preferred_element_type=jnp.float32)
        + gru_in_bias
    )
    from_state = jnp.dot(state_bf, gru_hidden, preferred_element_type=jnp.float32) + gru_hid_bias
    reset = jax.nn.sigmoid(from_input[:, :row_width] + from_state[:, :row_width])
    update = jax.nn.sigmoid(
        from_input[:, row_width : 2 * row_width] + from_state[:, row_width : 2 * row_width]
    )
    candidate = jnp.tanh(from_input[:, 2 * row_width :] + reset * from_state[:, 2 * row_width :])
    return (1.0 - update) * candidate + update * old_state


def look_up(table, ids):
    width = 128
    groups = table.shape[0] // width
    grid = table.reshape(groups, width)
    digits = jnp.concatenate([grid >> 8, grid & 255], 1).astype(jnp.bfloat16)
    pick = ((ids // width)[..., None] == jnp.arange(groups, dtype=jnp.int32)).astype(jnp.bfloat16)
    rows = jnp.dot(pick, digits, preferred_element_type=jnp.float32)
    here = (ids % width)[..., None] == jnp.arange(width, dtype=jnp.int32)
    both = jnp.where(here, rows[..., :width] * 256.0 + rows[..., width:], 0.0)
    return jnp.sum(both, -1).astype(jnp.int32)


def sum_everywhere(gradients, loss_local, count_local, devices):
    g_self, g_nbr, g_embed, g_dec1, g_bias1, g_dec2, g_bias2 = gradients
    width = g_self.shape[1]
    scalars = jnp.concatenate([g_bias2, loss_local[None], count_local[None]])
    scalars = jnp.pad(scalars, (0, width - scalars.shape[0]))
    table = jnp.concatenate(
        [g_self, g_nbr, g_dec1, jnp.stack([g_embed, g_bias1, g_dec2, scalars])], 0
    )
    used = table.shape[0]
    share = -(-used // (devices * 8)) * 8
    table = jnp.pad(table, ((0, share * devices - used), (0, 0))).reshape(devices, share, width)
    parts = lax.all_to_all(table, ("mem", "rep"), split_axis=0, concat_axis=0, tiled=True)
    total = lax.all_gather(jnp.sum(parts, 0), ("mem", "rep"), axis=0, tiled=True)
    n_self, n_nbr, n_dec1 = (g_self.shape[0], g_nbr.shape[0], g_dec1.shape[0])
    at = n_self + n_nbr + n_dec1
    return (
        (
            total[:n_self],
            total[n_self : n_self + n_nbr],
            total[at],
            total[n_self + n_nbr : at],
            total[at + 1],
            total[at + 2],
            total[at + 3, :1],
        ),
        total[at + 3, 1],
        total[at + 3, 2],
    )


def place_rows(owner_ids, owners, stride, offset):
    length = owner_ids.shape[0]
    width = 128
    groups = -(-length // width)
    padded_ids = owner_ids.reshape(groups, width)
    one_hot = (padded_ids[:, :, None] == jnp.arange(owners, dtype=jnp.int32)[None, None, :]).astype(
        jnp.float32
    )
    lower = (
        jnp.arange(width, dtype=jnp.int32)[:, None] > jnp.arange(width, dtype=jnp.int32)[None, :]
    ).astype(jnp.float32)
    within = jnp.einsum("ij,gjo->gio", lower, one_hot, precision=lax.Precision.HIGHEST)
    totals = jnp.sum(one_hot, 1)
    starts = jnp.cumsum(totals, 0) - totals
    before = jnp.sum((within + starts[:, None, :]) * one_hot, 2).reshape(-1)
    return owner_ids * stride + offset + before.astype(jnp.int32)


def body(
    memory,
    node_slot,
    event_nodes,
    event_times,
    valid_mask,
    time_freq,
    time_phase,
    gru_input,
    gru_hidden,
    gru_in_bias,
    gru_hid_bias,
    w_self,
    w_nbr,
    b_embed,
    w_dec1,
    b_dec1,
    w_dec2,
    b_dec2,
):
    owners = lax.axis_size("mem")
    devices = owners * lax.axis_size("rep")
    node_dev, row_width = memory.shape
    batches, events, columns = event_nodes.shape
    neighbours = (columns - 3) // 3
    cap_pair = 2 * events // owners * 2
    params = (w_self, w_nbr, b_embed, w_dec1, b_dec1, w_dec2, b_dec2)
    losses = []
    all_slots = look_up(node_slot, event_nodes.transpose(0, 2, 1))
    for batch_index in range(batches):
        slot_ids = all_slots[batch_index]
        memory_bf = memory.astype(jnp.bfloat16)
        whole_bf = lax.all_gather(memory_bf, "mem", axis=0, tiled=True)
        fetched = jnp.take(whole_bf, slot_ids.reshape(-1), axis=0, mode="clip")
        own_rows = fetched[: 3 * events]
        beside = fetched[3 * events :].reshape(3, neighbours, events, row_width)
        beside_sum = jnp.sum(beside.astype(jnp.float32), 1).reshape(3 * events, row_width)
        pair_slots = slot_ids[:2].reshape(-1)
        pair_at = place_rows(pair_slots // node_dev, owners, cap_pair, 0)
        offsets = (pair_slots % node_dev).astype(jnp.int32)
        time_code = jnp.cos(
            event_times[batch_index].astype(jnp.float32)[:, None] * time_freq + time_phase
        ).astype(jnp.bfloat16)
        marks = jnp.stack([jnp.ones_like(offsets), offsets // 128, offsets % 128], 1)
        partners = jnp.concatenate([own_rows[events : 2 * events], own_rows[:events]], 0)
        letters = jnp.concatenate(
            [partners, jnp.concatenate([time_code, time_code], 0), marks.astype(jnp.bfloat16)], 1
        )
        seats = jnp.arange(owners * cap_pair, dtype=jnp.int32)[:, None] == pair_at[None, :]
        parcel = jnp.dot(
            seats.astype(jnp.bfloat16), letters, preferred_element_type=jnp.float32
        ).astype(jnp.bfloat16)
        parcel = parcel.reshape(owners, cap_pair, letters.shape[1])
        parcel = lax.all_to_all(parcel, "mem", split_axis=0, concat_axis=0, tiled=True)
        every_parcel = lax.all_gather(parcel, "rep", axis=0, tiled=True)
        every_parcel = every_parcel.reshape(-1, letters.shape[1])
        digits = every_parcel[:, -2:].astype(jnp.int32)
        target = digits[:, 0] * 128 + digits[:, 1]
        matches = jnp.arange(node_dev, dtype=jnp.int32)[:, None] == target[None, :]
        summed = jnp.dot(
            matches.astype(jnp.bfloat16), every_parcel, preferred_element_type=jnp.float32
        )
        counts = summed[:, -3:-2]
        mean_rest = (summed[:, :-3] / jnp.maximum(counts, 1.0)).astype(jnp.bfloat16)
        fresh = memory_update(
            mean_rest, memory_bf, memory, gru_input, gru_hidden, gru_in_bias, gru_hid_bias
        )
        memory = jnp.where(counts > 0, fresh, memory)
        valid_part = valid_mask[batch_index]
        loss_local, pullback = jax.vjp(
            lambda current: block_loss(current, own_rows, beside_sum, neighbours, valid_part),
            params,
        )
        gradients = pullback(jnp.ones_like(loss_local))[0]
        count_local = jnp.sum(valid_part.astype(jnp.float32))
        gradients, loss_total, count_total = sum_everywhere(
            gradients, loss_local, count_local, devices
        )
        params = normalized_step(params, gradients)
        losses.append(loss_total / jnp.maximum(count_total, 1.0))
    return (
        memory,
        jnp.stack(losses),
        params[0],
        params[1],
        params[2],
        params[3],
        params[4],
        params[5],
        params[6],
    )


def solution(mesh):
    return jax.shard_map(
        body,
        mesh=mesh,
        in_specs=(
            P("mem", None),
            P(),
            P(None, ("mem", "rep"), None),
            P(None, ("mem", "rep")),
            P(None, ("mem", "rep")),
            P(),
            P(),
            P(),
            P(),
            P(),
            P(),
            P(),
            P(),
            P(),
            P(),
            P(),
            P(),
            P(),
        ),
        out_specs=(P("mem", None), P(), P(), P(), P(), P(), P(), P(), P()),
        check_vma=False,
    )
```

profile of v0, /device:TPU:0, one launch (start us, length us, event | category | flops | bytes accessed | tf_op | source)
XLA Modules:
  0.0 355.3 jit_solution(9725286313087995322)
XLA Ops:
  7.2 2.2 copy.57
  9.5 0.9 and_select_fusion.1
  10.4 0.8 fusion.114
  11.2 1.3 fusion.6
  12.5 3.1 fusion.3
  17.5 0.8 fusion.78
  18.3 67.9 %all-gather.5.cloned.1.call-done = bf16[8192,172]{1,0:T(8,128)(2,1)} async-done(((bf16[1024,172]{1,0:T(8,128)(2,1)}), bf16[8192,172]{1,0:T(8,128)(2,1)}) %all-gather.5.cloned.1.call-update) | async-done | bytes 2818064 | tf_op jit(solution)/shard_map/all_gather | solution.py:146
  86.3 12.3 %gather_fusion = bf16[4224,172]{1,0:T(8,128)(2,1)S(1)} fusion(bf16[8192,172]{1,0:T(8,128)(2,1)} %all-gather.5.cloned.1.call-done, s32[5120]{0:T(1024)S(1)} %pad_clamp_fusion.1), kind=kCustom, calls=%fused_computation | custom fusion | bytes 2923008 | tf_op jit(solution)/shard_map/jit(_take)/gather | solution.py:147
  98.7 1.1 concatenate.69
  99.8 1.0 convolution_convert_fusion.1
  100.8 1.2 copy.61
  102.0 15.1 %all_to_all.20 = bf16[8,64,275]{2,1,0:T(8,128)(2,1)} all-to-all(bf16[8,64,275]{2,1,0:T(8,128)(2,1)S(1)} %bitcast.175), channel_id=1, replica_groups=mesh['mem'=8,'rep'=4] {'mem'}, dimensions={0} | all-to-all | bytes 563200 | tf_op jit(solution)/shard_map/all_to_all | solution.py:167
  117.4 1.8 convolution_add_fusion
  119.2 1.8 fusion.66
  121.0 14.4 %all-gather.7.cloned.1.call-done = bf16[32,64,275]{2,1,0:T(8,128)(2,1)} async-done(((bf16[8,64,275]{2,1,0:T(8,128)(2,1)}), bf16[32,64,275]{2,1,0:T(8,128)(2,1)}) %all-gather.7.cloned.1.call-update) | async-done | bytes 1126416 | tf_op jit(solution)/shard_map/all_gather | solution.py:168
  135.5 1.4 slice_convert_fusion.1
  136.9 0.6 fusion.29
  137.6 2.0 fusion.1
  139.6 0.8 add_add_fusion.1
  140.4 0.8 copy-done.1
  141.4 1.6 fusion.145
  146.7 0.6 fusion.143
  147.8 2.0 fusion.127
  150.5 0.8 fusion.18
  151.5 0.8 pad.29
  152.3 4.6 %all-to-all-start.2 = ((f32[32,24,100]{2,1,0:T(8,128)}), f32[32,24,100]{2,1,0:T(8,128)S(1)}, u32[]{:S(2)}, u32[]{:S(2)}) async-start(f32[32,24,100]{2,1,0:T(8,128)} %bitcast.37), calls=%async_computation.2 | async-start | bytes 786432 | tf_op jit(solution)/shard_map/all_to_all | solution.py:77
  157.1 0.8 fusion.81
  157.9 18.0 %all-to-all-done.2 = f32[32,24,100]{2,1,0:T(8,128)S(1)} async-done(((f32[32,24,100]{2,1,0:T(8,128)}), f32[32,24,100]{2,1,0:T(8,128)S(1)}, u32[]{:S(2)}, u32[]{:S(2)}) %all-to-all-start.2) | async-done | bytes 307232 | tf_op jit(solution)/shard_map/all_to_all | solution.py:77
  175.9 42.3 %all_gather.22 = f32[768,100]{1,0:T(8,128)S(1)} all-gather(f32[24,100]{1,0:T(8,128)S(1)} %reduce_sum.364), channel_id=1, replica_groups=mesh['mem'=8,'rep'=4] {'mem','rep'}, dimensions={0}, use_global_device_ids=true | all-gather | bytes 316800 | tf_op jit(solution)/shard_map/all_gather | solution.py:78
  218.2 0.6 fusion.150
  220.1 0.6 multiply_reduce_fusion.8
  222.0 0.6 multiply_reduce_fusion.15
  223.3 0.6 multiply_reduce_fusion.5
  226.7 5.8 %copy.62 = bf16[8192,172]{1,0:T(8,128)(2,1)} copy(bf16[8192,172]{0,1:T(8,128)(2,1)} %all-gather.9.cloned.1.call-done) | data formatting | bytes 5636096 | tf_op jit(solution)/shard_map/all_gather | solution.py:146
  232.5 12.3 %gather_fusion.1 = bf16[4224,172]{1,0:T(8,128)(2,1)S(1)} fusion(bf16[8192,172]{1,0:T(8,128)(2,1)} %copy.62, s32[5120]{0:T(1024)S(1)} %pad_clamp_fusion), kind=kCustom, calls=%fused_computation.1 | custom fusion | bytes 2923008 | tf_op jit(solution)/shard_map/jit(_take)/gather | solution.py:147
  245.6 1.1 fusion.153
  246.9 0.6 fusion.141
  247.5 0.7 multiply_reduce_fusion
  248.5 0.6 split.29
  249.8 0.9 fusion.13
  250.7 1.7 concatenate.72
  252.4 1.2 convolution_convert_fusion
  253.7 0.9 copy.66
  254.6 4.2 %all-to-all-start.1 = ((bf16[8,64,275]{2,1,0:T(8,128)(2,1)}), bf16[8,64,275]{2,1,0:T(8,128)(2,1)}, u32[]{:S(2)}, u32[]{:S(2)}) async-start(bf16[8,64,275]{2,1,0:T(8,128)(2,1)} %bitcast.174), calls=%async_computation.1 | async-start | bytes 786432 | tf_op jit(solution)/shard_map/all_to_all | solution.py:167
  258.8 1.1 fusion.140
  259.9 2.0 fusion.126
  261.9 1.8 fusion.15
  263.7 1.8 fusion.17
  265.5 2.0 concatenate.86
  267.5 0.8 pad.33
  268.3 3.0 all-to-all-done.1
  271.3 2.7 all-to-all-start.3
  275.2 1.8 fusion.64
  277.6 9.7 %all-to-all-done.3 = f32[32,24,100]{2,1,0:T(8,128)S(1)} async-done(((f32[32,24,100]{2,1,0:T(8,128)}), f32[32,24,100]{2,1,0:T(8,128)S(1)}, u32[]{:S(2)}, u32[]{:S(2)}) %all-to-all-start.3) | async-done | bytes 307232 | tf_op jit(solution)/shard_map/all_to_all | solution.py:77
  287.3 39.6 %all_gather.23 = f32[768,100]{1,0:T(8,128)S(1)} all-gather(f32[24,100]{1,0:T(8,128)S(1)} %reduce_sum.380), channel_id=1, replica_groups=mesh['mem'=8,'rep'=4] {'mem','rep'}, dimensions={0}, use_global_device_ids=true | all-gather | bytes 316800 | tf_op jit(solution)/shard_map/all_gather | solution.py:78
  328.8 0.6 multiply_reduce_fusion.6
  332.0 0.6 multiply_reduce_fusion.4
  337.7 1.6 multiply_subtract_fusion
  339.3 1.6 multiply_subtract_fusion.2
  340.9 1.4 slice_convert_fusion
  342.4 0.6 fusion.28
  343.0 2.0 fusion
  345.1 0.8 add_add_fusion
  346.2 1.4 fusion.34
  (151 shorter events, 12.1 us)
Async XLA Ops:
  7.2 110.2 %copy-start = (bf16[172,516]{1,0:T(8,128)(2,1)S(1)}, bf16[172,516]{1,0:T(8,128)(2,1)}, u32[]{:S(2)}) copy-start(bf16[172,516]{1,0:T(8,128)(2,1)} %param.27) | copy-start | bytes 532516
  7.2 79.1 %all-gather.5.cloned.1.call-start = ((), (), s32[]{:S(2)}) async-start(), calls=%async_computation.4 | async-start | bytes 4718592 | tf_op jit(solution)/shard_map/all_gather | solution.py:146
  9.4 126.0 %all-gather.7.cloned.1.call-start = ((), (), s32[]{:S(2)}) async-start(), calls=%async_computation.5 | async-start | bytes 1966080 | tf_op jit(solution)/shard_map/all_gather | solution.py:168
  12.5 3.9 %copy-start.33 = (s32[2,128]{1,0:T(2,128)S(1)}, s32[2,128]{1,0:T(2,128)}, u32[]{:S(2)}) copy-start(s32[2,128]{1,0:T(2,128)} %param.22) | copy-start | bytes 3076
  12.5 3.9 %copy-start.34 = (f32[100]{0:T(128)S(1)}, f32[100]{0:T(128)}, u32[]{:S(2)}) copy-start(f32[100]{0:T(128)} %param.25) | copy-start | bytes 1204
  12.5 3.9 %copy-start.35 = (f32[100]{0:T(128)S(1)}, f32[100]{0:T(128)}, u32[]{:S(2)}) copy-start(f32[100]{0:T(128)} %param.24) | copy-start | bytes 1204
  98.6 18.8 %copy-start.2 = (bf16[1024,172]{1,0:T(8,128)(2,1)S(1)}, bf16[1024,172]{1,0:T(8,128)(2,1)}, u32[]{:S(2)}) copy-start(bf16[1024,172]{1,0:T(8,128)(2,1)} %copy.57) | copy-start | bytes 1056772
  98.6 18.8 %copy-start.17 = (f32[516]{0:T(1024)S(1)}, f32[516]{0:T(1024)}, u32[]{:S(2)}) copy-start(f32[516]{0:T(1024)} %param.29) | copy-start | bytes 6196
  117.1 109.6 %all-gather.9.cloned.1.call-start = ((), (), s32[]{:S(2)}) async-start(), calls=%async_computation.6 | async-start | bytes 3244032 | tf_op jit(solution)/shard_map/all_gather | solution.py:146
  117.4 1.9 copy-start.11
  135.5 2.1 copy-start.16
  137.5 2.1 copy-start.6
  137.5 2.1 copy-start.12
  137.5 2.1 copy-start.37
  139.6 1.6 copy-start.1
  139.6 1.7 copy-start.5
  141.4 2.3 copy-start.26
  144.9 0.9 copy-start.9
  144.9 1.1 copy-start.10
  144.9 1.1 copy-start.27
  145.0 1.5 copy-start.8
  145.0 1.5 copy-start.19
  145.0 1.5 copy-start.36
  145.0 1.7 copy-start.24
  152.3 23.5 %all-to-all-start.2 = ((f32[32,24,100]{2,1,0:T(8,128)}), f32[32,24,100]{2,1,0:T(8,128)S(1)}, u32[]{:S(2)}, u32[]{:S(2)}) async-start(f32[32,24,100]{2,1,0:T(8,128)} %bitcast.37), calls=%async_computation.2 | async-start | bytes 786432 | tf_op jit(solution)/shard_map/all_to_all | solution.py:77
  226.6 19.0 %copy-start.22 = (f32[100]{0:T(128)}, f32[100]{0:T(128)S(1)}, u32[]{:S(2)}) copy-start(f32[100]{0:T(128)S(1)} %get-tuple-element.57) | copy-start | bytes 1204
  226.6 20.0 %copy-start.28 = (f32[100]{0:T(128)}, f32[100]{0:T(128)S(1)}, u32[]{:S(2)}) copy-start(f32[100]{0:T(128)S(1)} %get-tuple-element.58) | copy-start | bytes 1204
  226.6 23.1 %copy-start.20 = (f32[100]{0:T(128)}, f32[100]{0:T(128)S(1)}, u32[]{:S(2)}) copy-start(f32[100]{0:T(128)S(1)} %get-tuple-element.56) | copy-start | bytes 1204
  245.2 1.7 copy-start.25
  245.2 1.7 copy-start.30
  250.7 14.8 %copy-start.31 = (f32[100]{0:T(128)S(1)}, f32[100]{0:T(128)}, u32[]{:S(2)}) copy-start(f32[100]{0:T(128)} %get-tuple-element.29) | copy-start | bytes 1204
  250.7 14.8 %copy-start.32 = (f32[100]{0:T(128)S(1)}, f32[100]{0:T(128)}, u32[]{:S(2)}) copy-start(f32[100]{0:T(128)} %get-tuple-element.30) | copy-start | bytes 1204
  254.6 20.6 %copy-start.3 = (bf16[1024,172]{0,1:T(8,128)(2,1)S(1)}, bf16[1024,172]{0,1:T(8,128)(2,1)}, u32[]{:S(2)}) copy-start(bf16[1024,172]{0,1:T(8,128)(2,1)} %get-tuple-element.39) | copy-start | bytes 1056772
  254.6 16.7 %all-to-all-start.1 = ((bf16[8,64,275]{2,1,0:T(8,128)(2,1)}), bf16[8,64,275]{2,1,0:T(8,128)(2,1)}, u32[]{:S(2)}, u32[]{:S(2)}) async-start(bf16[8,64,275]{2,1,0:T(8,128)(2,1)} %bitcast.174), calls=%async_computation.1 | async-start | bytes 786432 | tf_op jit(solution)/shard_map/all_to_all | solution.py:167
  263.7 11.5 %copy-start.13 = (bf16[444,516]{0,1:T(8,128)(2,1)S(1)}, bf16[444,516]{0,1:T(8,128)(2,1)}, u32[]{:S(2)}) copy-start(bf16[444,516]{0,1:T(8,128)(2,1)} %param.26) | copy-start | bytes 1374628
  268.3 8.8 %copy-start.18 = (f32[516]{0:T(1024)S(1)}, f32[516]{0:T(1024)}, u32[]{:S(2)}) copy-start(f32[516]{0:T(1024)} %param.29) | copy-start | bytes 6196
  271.3 16.0 %all-to-all-start.3 = ((f32[32,24,100]{2,1,0:T(8,128)}), f32[32,24,100]{2,1,0:T(8,128)S(1)}, u32[]{:S(2)}, u32[]{:S(2)}) async-start(f32[32,24,100]{2,1,0:T(8,128)} %bitcast.56), calls=%async_computation.3 | async-start | bytes 786432 | tf_op jit(solution)/shard_map/all_to_all | solution.py:77
  274.0 66.9 %all-gather.11.cloned.1.call-start = ((), (), s32[]{:S(2)}) async-start(), calls=%async_computation.7 | async-start | bytes 1966080 | tf_op jit(solution)/shard_map/all_gather | solution.py:168
  277.0 60.2 %copy-start.21 = (f32[100]{0:T(128)S(1)}, f32[100]{0:T(128)}, u32[]{:S(2)}) copy-start(f32[100]{0:T(128)} %copy-done.20) | copy-start | bytes 1204
  277.0 60.2 %copy-start.23 = (f32[100]{0:T(128)S(1)}, f32[100]{0:T(128)}, u32[]{:S(2)}) copy-start(f32[100]{0:T(128)} %copy-done.22) | copy-start | bytes 1204
  277.0 60.2 %copy-start.29 = (f32[100]{0:T(128)S(1)}, f32[100]{0:T(128)}, u32[]{:S(2)}) copy-start(f32[100]{0:T(128)} %copy-done.28) | copy-start | bytes 1204
  340.9 2.1 copy-start.15
  343.0 2.1 copy-start.7
  343.0 2.1 copy-start.14
  343.0 2.1 copy-start.38
  345.1 1.1 copy-start.4
Sparse Core Ops, SparseCore 0:
  10.7 75.5 all-gather.4
  117.2 18.1 all-gather.6
  143.1 65.9 all-gather.8
  277.2 21.7 all-gather.10
where the time goes:
time: 357 us; the launch traced here: 355 us
  waiting for transfers between devices  113 us (32%)
  blocking collectives  97 us (27%)
  local copies, waits for them, and re-layouts  45.8 us (13%)
  other arithmetic  32.9 us (9%)
  between operations  30.8 us (9%)
  matrix products  23.9 us (7%)
  starting transfers between devices  11.9 us (3%)
    all_gather x2, blocking collectives, sum_everywhere(): lax.all_gather(jnp.sum(parts, 0), ('mem', 'rep'), axis=0, tiled=True)  81.9 us
    all_gather x2, waiting for transfers between devices, body(): whole_bf = lax.all_gather(memory_bf, 'mem', axis=0, tiled=True)  67.9 us
    all_to_all x2, waiting for transfers between devices, sum_everywhere(): lax.all_to_all(table, ('mem', 'rep'), split_axis=0, concat_axis=0, tiled=...  27.7 us
    gather x2, local copies, waits for them, and re-layouts, body(): fetched = jnp.take(whole_bf, slot_ids.reshape(-1), axis=0, mode='clip')  24.7 us
    all_to_all x1, blocking collectives, body(): lax.all_to_all(parcel, 'mem', split_axis=0, concat_axis=0, tiled=True)  15.1 us
    all_gather x2, waiting for transfers between devices, body(): every_parcel = lax.all_gather(parcel, 'rep', axis=0, tiled=True)  14.4 us
    all_to_all x2, starting transfers between devices, sum_everywhere(): lax.all_to_all(table, ('mem', 'rep'), split_axis=0, concat_axis=0, tiled=...  7.3 us
  transfers between devices with their start and end apart: 7, of which 5 were waited for; matrix products, arithmetic and copies ran while one was open for 12% of the time, Pallas kernels for 0%

commit v1 on v0

--- a/solution.py
+++ b/solution.py
@@ -4,6 +4,17 @@
 from jax.sharding import PartitionSpec as P
 
 step_size = 4.0
+
+
+def around_the_ring(block, mesh_axis, dim):
+    peers = lax.axis_size(mesh_axis)
+    right = [(i, (i + 1) % peers) for i in range(peers)]
+    parts = [block]
+    for far in range(1, peers):
+        parts = [lax.ppermute(parts[0], mesh_axis, right), *parts]
+    whole = jnp.concatenate(parts, axis=dim)
+    shift = (lax.axis_index(mesh_axis) + 1) * parts[-1].shape[dim]
+    return jnp.roll(whole, shift, axis=dim)
 
 
 def block_loss(current, own_rows, beside_sum, neighbours, valid_part):
@@ -143,7 +154,7 @@
     for batch_index in range(batches):
         slot_ids = all_slots[batch_index]
         memory_bf = memory.astype(jnp.bfloat16)
-        whole_bf = lax.all_gather(memory_bf, "mem", axis=0, tiled=True)
+        whole_bf = around_the_ring(memory_bf, "mem", 0)
         fetched = jnp.take(whole_bf, slot_ids.reshape(-1), axis=0, mode="clip")
         own_rows = fetched[: 3 * events]
         beside = fetched[3 * events :].reshape(3, neighbours, events, row_width)

time: 357 us -> 440 us (1.23)
  waiting for transfers between devices: 113 us -> 166 us
  other arithmetic: 32.9 us -> 54.4 us
  blocking collectives: 97 us -> 82.6 us
  starting transfers between devices: 11.9 us -> 23.8 us
  local copies, waits for them, and re-layouts: 45.8 us -> 53.6 us
    ppermute x0 -> x14, waiting for transfers between devices: none -> 138 us  [around_the_ring(): parts = [lax.ppermute(parts[0], mesh_axis, right), *parts]]
    all_gather x2 -> x0, waiting for transfers between devices: 67.9 us -> none  [body(): whole_bf = lax.all_gather(memory_bf, 'mem', axis=0, tiled=True)]
    all_to_all x2, waiting for transfers between devices: 27.7 us -> 9.99 us  [sum_everywhere(): lax.all_to_all(table, ('mem', 'rep'), split_axis=0, concat_axis=0, tiled=...]
    all_to_all x1 -> x0, blocking collectives: 15.1 us -> none  [body(): lax.all_to_all(parcel, 'mem', split_axis=0, concat_axis=0, tiled=True)]
    concatenate x0 -> x2, other arithmetic: none -> 14.9 us  [around_the_ring(): return jnp.roll(whole, shift, axis=dim)]
    all_gather x1 -> x0, local copies, waits for them, and re-layouts: 5.81 us -> none  [body(): whole_bf = lax.all_gather(memory_bf, 'mem', axis=0, tiled=True)]
    ppermute x0 -> x14, starting transfers between devices: none -> 5.11 us  [around_the_ring(): parts = [lax.ppermute(parts[0], mesh_axis, right), *parts]]
    unnamed x79 -> x111, local copies, waits for them, and re-layouts: 4.12 us -> 8.9 us
  transfers between devices with their start and end apart: 7 -> 20, of which waited for: 5 -> 17; matrix products, arithmetic and copies ran while one was open for 12% -> 13% of each run, Pallas kernels for 0% -> 0%
where the time goes in v1:
time: 440 us; the launch traced here: 438 us
  waiting for transfers between devices  166 us (38%)
  blocking collectives  82.6 us (19%)
  other arithmetic  54.4 us (12%)
  local copies, waits for them, and re-layouts  53.6 us (12%)
  between operations  31.3 us (7%)
  matrix products  26.2 us (6%)
  starting transfers between devices  23.8 us (5%)
    ppermute x14, waiting for transfers between devices, around_the_ring(): parts = [lax.ppermute(parts[0], mesh_axis, right), *parts]  138 us
    all_gather x2, blocking collectives, sum_everywhere(): lax.all_gather(jnp.sum(parts, 0), ('mem', 'rep'), axis=0, tiled=True)  82.6 us
    gather x2, local copies, waits for them, and re-layouts, body(): fetched = jnp.take(whole_bf, slot_ids.reshape(-1), axis=0, mode='clip')  24.8 us
    concatenate x2, other arithmetic, around_the_ring(): return jnp.roll(whole, shift, axis=dim)  14.9 us
    all_gather x2, waiting for transfers between devices, body(): every_parcel = lax.all_gather(parcel, 'rep', axis=0, tiled=True)  12.8 us
    all_to_all x2, starting transfers between devices, sum_everywhere(): lax.all_to_all(table, ('mem', 'rep'), split_axis=0, concat_axis=0, tiled=...  10.8 us
    all_to_all x2, waiting for transfers between devices, sum_everywhere(): lax.all_to_all(table, ('mem', 'rep'), split_axis=0, concat_axis=0, tiled=...  9.99 us
    unnamed x111, local copies, waits for them, and re-layouts  8.9 us
  transfers between devices with their start and end apart: 20, of which 17 were waited for; matrix products, arithmetic and copies ran while one was open for 13% of the time, Pallas kernels for 0%

profile of v1, /device:TPU:0, one launch (start us, length us, event | category | flops | bytes accessed | tf_op | source)
XLA Modules:
  0.0 438.0 jit_solution(1663895596164415834)
XLA Ops:
  7.2 1.4 copy.57
  8.5 3.0 collective-permute-start
  11.6 0.9 and_select_fusion.1
  13.2 1.3 fusion.8
  14.6 11.9 %collective-permute-done = bf16[1024,172]{1,0:T(8,128)(2,1)S(1)} collective-permute-done((bf16[1024,172]{1,0:T(8,128)(2,1)S(1)}, bf16[1024,172]{1,0:T(8,128)(2,1)S(1)}, u32[]{:S(2)}, u32[]{:S(2)}) %collective-permute-start) | collective-permute-done | bytes 352288 | tf_op jit(solution)/shard_map/ppermute | solution.py:14
  26.5 3.1 fusion.3
  29.6 12.7 %collective-permute-done.1 = bf16[1024,172]{1,0:T(8,128)(2,1)S(1)} collective-permute-done((bf16[1024,172]{1,0:T(8,128)(2,1)S(1)}, bf16[1024,172]{1,0:T(8,128)(2,1)S(1)}, u32[]{:S(2)}, u32[]{:S(2)}) %collective-permute-start.1) | collective-permute-done | bytes 352288 | tf_op jit(solution)/shard_map/ppermute | solution.py:14
  42.8 14.4 %collective-permute-done.2 = bf16[1024,172]{1,0:T(8,128)(2,1)S(1)} collective-permute-done((bf16[1024,172]{1,0:T(8,128)(2,1)S(1)}, bf16[1024,172]{1,0:T(8,128)(2,1)S(1)}, u32[]{:S(2)}, u32[]{:S(2)}) %collective-permute-start.2) | collective-permute-done | bytes 352288 | tf_op jit(solution)/shard_map/ppermute | solution.py:14
  58.4 12.9 %collective-permute-done.3 = bf16[1024,172]{1,0:T(8,128)(2,1)S(1)} collective-permute-done((bf16[1024,172]{1,0:T(8,128)(2,1)S(1)}, bf16[1024,172]{1,0:T(8,128)(2,1)S(1)}, u32[]{:S(2)}, u32[]{:S(2)}) %collective-permute-start.3) | collective-permute-done | bytes 352288 | tf_op jit(solution)/shard_map/ppermute | solution.py:14
  71.4 0.9 cosine_convert_fusion
  72.3 12.3 %collective-permute-done.4 = bf16[1024,172]{1,0:T(8,128)(2,1)S(1)} collective-permute-done((bf16[1024,172]{1,0:T(8,128)(2,1)S(1)}, bf16[1024,172]{1,0:T(8,128)(2,1)S(1)}, u32[]{:S(2)}, u32[]{:S(2)}) %collective-permute-start.4) | collective-permute-done | bytes 352288 | tf_op jit(solution)/shard_map/ppermute | solution.py:14
  85.9 1.5 pad_maximum_fusion.4
  88.3 8.7 %collective-permute-done.5 = bf16[1024,172]{1,0:T(8,128)(2,1)} collective-permute-done((bf16[1024,172]{1,0:T(8,128)(2,1)S(1)}, bf16[1024,172]{1,0:T(8,128)(2,1)}, u32[]{:S(2)}, u32[]{:S(2)}) %collective-permute-start.5) | collective-permute-done | bytes 352288 | tf_op jit(solution)/shard_map/ppermute | solution.py:14
  97.7 2.5 convolution_add_fusion
  100.2 9.0 %collective-permute-done.6 = bf16[1024,172]{1,0:T(8,128)(2,1)} collective-permute-done((bf16[1024,172]{1,0:T(8,128)(2,1)}, bf16[1024,172]{1,0:T(8,128)(2,1)}, u32[]{:S(2)}, u32[]{:S(2)}) %collective-permute-start.6) | collective-permute-done | bytes 352288 | tf_op jit(solution)/shard_map/ppermute | solution.py:14
  109.2 1.1 constant_dynamic-update-slice_fusion.7
  110.3 1.1 constant_dynamic-update-slice_fusion.6
  111.6 13.4 %fusion.4 = bf16[8192,172]{1,0:T(8,128)(2,1)} fusion(s32[]{:T(128)S(6)} %select_n.172, bf16[8192,172]{1,0:T(8,128)(2,1)S(1)} %constant_dynamic-update-slice_fusion), kind=kLoop, calls=%fused_computation.15 | loop fusion | flops 5636096 | bytes 5636100 | tf_op jit(solution)/shard_map/jit(_roll_dynamic)/concatenate | solution.py:17
  125.0 12.4 %gather_fusion = bf16[4224,172]{1,0:T(8,128)(2,1)S(1)} fusion(bf16[8192,172]{1,0:T(8,128)(2,1)} %fusion.4, s32[5120]{0:T(1024)S(1)} %pad_clamp_fusion.1), kind=kCustom, calls=%fused_computation | custom fusion | bytes 2923008 | tf_op jit(solution)/shard_map/jit(_take)/gather | solution.py:158
  138.5 0.9 copy.61
  139.4 3.5 all-to-all-start
  143.7 2.8 fusion.68
  146.4 5.6 %all-to-all-done = bf16[8,64,275]{2,1,0:T(8,128)(2,1)S(1)} async-done(((bf16[8,64,275]{2,1,0:T(8,128)(2,1)}), bf16[8,64,275]{2,1,0:T(8,128)(2,1)S(1)}, u32[]{:S(2)}, u32[]{:S(2)}) %all-to-all-start) | async-done | bytes 281632 | tf_op jit(solution)/shard_map/all_to_all | solution.py:178
  157.6 12.8 %all-gather.3.cloned.1.call-done = bf16[32,64,275]{2,1,0:T(8,128)(2,1)} async-done(((bf16[8,64,275]{2,1,0:T(8,128)(2,1)}), bf16[32,64,275]{2,1,0:T(8,128)(2,1)}) %all-gather.3.cloned.1.call-update) | async-done | bytes 1126416 | tf_op jit(solution)/shard_map/all_gather | solution.py:179
  170.4 1.4 slice_convert_fusion.1
  172.5 2.0 fusion.1
  176.3 1.5 fusion.147
  177.8 1.5 collective-permute-start.7
  179.3 0.9 fusion.16
  180.2 10.9 %collective-permute-done.7 = bf16[1024,172]{0,1:T(8,128)(2,1)S(1)} collective-permute-done((bf16[1024,172]{0,1:T(8,128)(2,1)S(1)}, bf16[1024,172]{0,1:T(8,128)(2,1)S(1)}, u32[]{:S(2)}, u32[]{:S(2)}) %collective-permute-start.7) | collective-permute-done | bytes 352288 | tf_op jit(solution)/shard_map/ppermute | solution.py:14
  192.0 11.5 %collective-permute-done.8 = bf16[1024,172]{0,1:T(8,128)(2,1)} collective-permute-done((bf16[1024,172]{0,1:T(8,128)(2,1)S(1)}, bf16[1024,172]{0,1:T(8,128)(2,1)}, u32[]{:S(2)}, u32[]{:S(2)}) %collective-permute-start.8) | collective-permute-done | bytes 352288 | tf_op jit(solution)/shard_map/ppermute | solution.py:14
  203.5 2.0 fusion.129
  206.3 1.8 concatenate.90
  208.9 5.1 %all-to-all-start.2 = ((f32[32,24,100]{2,1,0:T(8,128)}), f32[32,24,100]{2,1,0:T(8,128)S(1)}, u32[]{:S(2)}, u32[]{:S(2)}) async-start(f32[32,24,100]{2,1,0:T(8,128)} %bitcast.37), calls=%async_computation.2 | async-start | bytes 786432 | tf_op jit(solution)/shard_map/all_to_all | solution.py:88
  214.0 1.2 collective-permute-done.9
  217.4 16.3 %collective-permute-done.10 = bf16[1024,172]{0,1:T(8,128)(2,1)S(1)} collective-permute-done((bf16[1024,172]{0,1:T(8,128)(2,1)S(1)}, bf16[1024,172]{0,1:T(8,128)(2,1)S(1)}, u32[]{:S(2)}, u32[]{:S(2)}) %collective-permute-start.10) | collective-permute-done | bytes 352288 | tf_op jit(solution)/shard_map/ppermute | solution.py:14
  233.7 0.8 fusion.83
  235.0 42.7 %all_gather.14 = f32[768,100]{1,0:T(8,128)S(1)} all-gather(f32[24,100]{1,0:T(8,128)S(1)} %reduce_sum.364), channel_id=1, replica_groups=mesh['mem'=8,'rep'=4] {'mem','rep'}, dimensions={0}, use_global_device_ids=true | all-gather | bytes 316800 | tf_op jit(solution)/shard_map/all_gather | solution.py:89
  286.2 4.9 %collective-permute-done.12 = bf16[1024,172]{0,1:T(8,128)(2,1)S(1)} collective-permute-done((bf16[1024,172]{0,1:T(8,128)(2,1)S(1)}, bf16[1024,172]{0,1:T(8,128)(2,1)S(1)}, u32[]{:S(2)}, u32[]{:S(2)}) %collective-permute-start.12) | collective-permute-done | bytes 352288 | tf_op jit(solution)/shard_map/ppermute | solution.py:14
  292.4 11.2 %collective-permute-done.13 = bf16[1024,172]{0,1:T(8,128)(2,1)S(1)} collective-permute-done((bf16[1024,172]{0,1:T(8,128)(2,1)S(1)}, bf16[1024,172]{0,1:T(8,128)(2,1)S(1)}, u32[]{:S(2)}, u32[]{:S(2)}) %collective-permute-start.13) | collective-permute-done | bytes 352288 | tf_op jit(solution)/shard_map/ppermute | solution.py:14
  303.7 1.0 constant_dynamic-update-slice_fusion.10
  304.8 1.5 fusion.7
  306.3 3.9 copy.62
  310.2 12.4 %gather_fusion.1 = bf16[4224,172]{1,0:T(8,128)(2,1)S(1)} fusion(bf16[8192,172]{1,0:T(8,128)(2,1)} %copy.62, s32[5120]{0:T(1024)S(1)} %pad_clamp_fusion), kind=kCustom, calls=%fused_computation.1 | custom fusion | bytes 2923008 | tf_op jit(solution)/shard_map/jit(_take)/gather | solution.py:158
  323.8 1.0 fusion.155
  327.9 0.9 fusion.15
  329.5 1.8 concatenate.83
  331.3 2.0 convolution_convert_fusion
  333.3 1.9 copy.66
  335.2 4.1 all-to-all-start.1
  339.3 1.6 fusion.142
  340.8 2.5 fusion.128
  343.3 1.8 fusion.17
  345.1 1.8 fusion.19
  346.9 2.7 concatenate.97
  350.4 5.7 %all-to-all-start.3 = ((f32[32,24,100]{2,1,0:T(8,128)}), f32[32,24,100]{2,1,0:T(8,128)S(1)}, u32[]{:S(2)}, u32[]{:S(2)}) async-start(f32[32,24,100]{2,1,0:T(8,128)} %bitcast.56), calls=%async_computation.3 | async-start | bytes 786432 | tf_op jit(solution)/shard_map/all_to_all | solution.py:88
  357.5 1.8 fusion.66
  359.8 9.5 %all-to-all-done.3 = f32[32,24,100]{2,1,0:T(8,128)S(1)} async-done(((f32[32,24,100]{2,1,0:T(8,128)}), f32[32,24,100]{2,1,0:T(8,128)S(1)}, u32[]{:S(2)}, u32[]{:S(2)}) %all-to-all-start.3) | async-done | bytes 307232 | tf_op jit(solution)/shard_map/all_to_all | solution.py:88
  369.4 39.9 %all_gather.15 = f32[768,100]{1,0:T(8,128)S(1)} all-gather(f32[24,100]{1,0:T(8,128)S(1)} %reduce_sum.380), channel_id=1, replica_groups=mesh['mem'=8,'rep'=4] {'mem','rep'}, dimensions={0}, use_global_device_ids=true | all-gather | bytes 316800 | tf_op jit(solution)/shard_map/all_gather | solution.py:89
  420.1 1.6 multiply_subtract_fusion
  421.7 1.6 multiply_subtract_fusion.2
  423.3 1.4 slice_convert_fusion
  425.4 2.0 fusion
  428.6 1.4 fusion.36
  (210 shorter events, 35.4 us)
Async XLA Ops:
  7.2 90.5 %copy-start = (bf16[172,516]{1,0:T(8,128)(2,1)S(1)}, bf16[172,516]{1,0:T(8,128)(2,1)}, u32[]{:S(2)}) copy-start(bf16[172,516]{1,0:T(8,128)(2,1)} %param.29) | copy-start | bytes 532516
  8.5 18.0 %collective-permute-start = (bf16[1024,172]{1,0:T(8,128)(2,1)S(1)}, bf16[1024,172]{1,0:T(8,128)(2,1)S(1)}, u32[]{:S(2)}, u32[]{:S(2)}) collective-permute-start(bf16[1024,172]{1,0:T(8,128)(2,1)S(1)} %copy.57), channel_id=1, source_target_pairs={{0,4},{4,8},{8,12},{12,16},{16,20},{20,24},{24,28},{28,0},{1,5},{5... | collective-permute-start | bytes 1056776 | tf_op jit(solution)/shard_map/ppermute | solution.py:14
  14.6 56.7 %copy-start.42 = (s32[2,128]{1,0:T(2,128)S(1)}, s32[2,128]{1,0:T(2,128)}, u32[]{:S(2)}) copy-start(s32[2,128]{1,0:T(2,128)} %param.24) | copy-start | bytes 3076
  14.6 56.7 %copy-start.43 = (f32[100]{0:T(128)S(1)}, f32[100]{0:T(128)}, u32[]{:S(2)}) copy-start(f32[100]{0:T(128)} %param.27) | copy-start | bytes 1204
  14.6 56.7 %copy-start.44 = (f32[100]{0:T(128)S(1)}, f32[100]{0:T(128)}, u32[]{:S(2)}) copy-start(f32[100]{0:T(128)} %param.26) | copy-start | bytes 1204
  26.5 15.8 %collective-permute-start.1 = (bf16[1024,172]{1,0:T(8,128)(2,1)S(1)}, bf16[1024,172]{1,0:T(8,128)(2,1)S(1)}, u32[]{:S(2)}, u32[]{:S(2)}) collective-permute-start(bf16[1024,172]{1,0:T(8,128)(2,1)S(1)} %collective-permute-done), channel_id=1, source_target_pairs={{0,4},{4,8},{8,12},{12,16},{16,20},{20,24},{24,28},{28,0},{1,5},{5... | collective-permute-start | bytes 1056776 | tf_op jit(solution)/shard_map/ppermute | solution.py:14
  42.3 14.9 %collective-permute-start.2 = (bf16[1024,172]{1,0:T(8,128)(2,1)S(1)}, bf16[1024,172]{1,0:T(8,128)(2,1)S(1)}, u32[]{:S(2)}, u32[]{:S(2)}) collective-permute-start(bf16[1024,172]{1,0:T(8,128)(2,1)S(1)} %collective-permute-done.1), channel_id=1, source_target_pairs={{0,4},{4,8},{8,12},{12,16},{16,20},{20,24},{24,28},{28,0},{1,5},{5... | collective-permute-start | bytes 1056776 | tf_op jit(solution)/shard_map/ppermute | solution.py:14
  57.2 14.1 %collective-permute-start.3 = (bf16[1024,172]{1,0:T(8,128)(2,1)S(1)}, bf16[1024,172]{1,0:T(8,128)(2,1)S(1)}, u32[]{:S(2)}, u32[]{:S(2)}) collective-permute-start(bf16[1024,172]{1,0:T(8,128)(2,1)S(1)} %collective-permute-done.2), channel_id=1, source_target_pairs={{0,4},{4,8},{8,12},{12,16},{16,20},{20,24},{24,28},{28,0},{1,5},{5... | collective-permute-start | bytes 1056776 | tf_op jit(solution)/shard_map/ppermute | solution.py:14
  71.3 13.2 %collective-permute-start.4 = (bf16[1024,172]{1,0:T(8,128)(2,1)S(1)}, bf16[1024,172]{1,0:T(8,128)(2,1)S(1)}, u32[]{:S(2)}, u32[]{:S(2)}) collective-permute-start(bf16[1024,172]{1,0:T(8,128)(2,1)S(1)} %collective-permute-done.3), channel_id=1, source_target_pairs={{0,4},{4,8},{8,12},{12,16},{16,20},{20,24},{24,28},{28,0},{1,5},{5... | collective-permute-start | bytes 1056776 | tf_op jit(solution)/shard_map/ppermute | solution.py:14
  84.5 12.5 %collective-permute-start.5 = (bf16[1024,172]{1,0:T(8,128)(2,1)S(1)}, bf16[1024,172]{1,0:T(8,128)(2,1)}, u32[]{:S(2)}, u32[]{:S(2)}) collective-permute-start(bf16[1024,172]{1,0:T(8,128)(2,1)S(1)} %collective-permute-done.4), channel_id=1, source_target_pairs={{0,4},{4,8},{8,12},{12,16},{16,20},{20,24},{24,28},{28,0},{1,5},{5... | collective-permute-start | bytes 1056776 | tf_op jit(solution)/shard_map/ppermute | solution.py:14
  97.0 12.2 %collective-permute-start.6 = (bf16[1024,172]{1,0:T(8,128)(2,1)}, bf16[1024,172]{1,0:T(8,128)(2,1)}, u32[]{:S(2)}, u32[]{:S(2)}) collective-permute-start(bf16[1024,172]{1,0:T(8,128)(2,1)} %collective-permute-done.5), channel_id=1, source_target_pairs={{0,4},{4,8},{8,12},{12,16},{16,20},{20,24},{24,28},{28,0},{1,5},{5... | collective-permute-start | bytes 1056776 | tf_op jit(solution)/shard_map/ppermute | solution.py:14
  125.0 12.5 %copy-start.22 = (bf16[256,100]{1,0:T(8,128)(2,1)S(1)}, bf16[256,100]{1,0:T(8,128)(2,1)}, u32[]{:S(2)}) copy-start(bf16[256,100]{1,0:T(8,128)(2,1)} %get-tuple-element.92) | copy-start | bytes 153604
  125.0 12.5 %copy-start.23 = (bf16[256,1]{1,0:T(8,128)(2,1)S(1)}, bf16[256,1]{1,0:T(8,128)(2,1)}, u32[]{:S(2)}) copy-start(bf16[256,1]{1,0:T(8,128)(2,1)} %get-tuple-element.62) | copy-start | bytes 1540
  125.0 12.5 %copy-start.24 = (bf16[256,1]{1,0:T(8,128)(2,1)S(1)}, bf16[256,1]{1,0:T(8,128)(2,1)}, u32[]{:S(2)}) copy-start(bf16[256,1]{1,0:T(8,128)(2,1)} %get-tuple-element.63) | copy-start | bytes 1540
  125.0 13.1 %copy-start.33 = (s32[256]{0:T(256)S(1)}, s32[256]{0:T(256)}, u32[]{:S(2)}) copy-start(s32[256]{0:T(256)} %get-tuple-element.65) | copy-start | bytes 3076
  137.4 5.7 %copy-start.36 = (s32[2,128]{1,0:T(2,128)S(1)}, s32[2,128]{1,0:T(2,128)}, u32[]{:S(2)}) copy-start(s32[2,128]{1,0:T(2,128)} %param.25) | copy-start | bytes 3076
  139.4 12.6 %all-to-all-start = ((bf16[8,64,275]{2,1,0:T(8,128)(2,1)}), bf16[8,64,275]{2,1,0:T(8,128)(2,1)S(1)}, u32[]{:S(2)}, u32[]{:S(2)}) async-start(bf16[8,64,275]{2,1,0:T(8,128)(2,1)} %bitcast.175), calls=%async_computation | async-start | bytes 786432 | tf_op jit(solution)/shard_map/all_to_all | solution.py:178
  142.9 27.5 %all-gather.3.cloned.1.call-start = ((), (), s32[]{:S(2)}) async-start(), calls=%async_computation.4 | async-start | bytes 1966080 | tf_op jit(solution)/shard_map/all_gather | solution.py:179
  153.4 1.1 copy-start.12
  153.4 1.1 copy-start.37
  153.6 1.4 copy-start.9
  153.6 1.4 copy-start.31
  153.6 1.4 copy-start.45
  153.6 1.6 copy-start.34
  155.0 1.7 copy-start.28
  170.4 2.1 copy-start.26
  172.4 2.1 copy-start.6
  172.4 2.1 copy-start.15
  172.5 2.1 copy-start.46
  174.5 1.6 copy-start.1
  174.5 1.7 copy-start.5
  176.3 3.0 copy-start.19
  176.3 3.0 copy-start.29
  177.8 13.2 %collective-permute-start.7 = (bf16[1024,172]{0,1:T(8,128)(2,1)S(1)}, bf16[1024,172]{0,1:T(8,128)(2,1)S(1)}, u32[]{:S(2)}, u32[]{:S(2)}) collective-permute-start(bf16[1024,172]{0,1:T(8,128)(2,1)S(1)} %get-tuple-element.40), channel_id=1, source_target_pairs={{0,4},{4,8},{8,12},{12,16},{16,20},{20,24},{24,28},{28,0},{1,5},{5... | collective-permute-start | bytes 1056776 | tf_op jit(solution)/shard_map/ppermute | solution.py:14
  191.0 15.3 %copy-start.20 = (bf16[1024,172]{0,1:T(8,128)(2,1)}, bf16[1024,172]{0,1:T(8,128)(2,1)S(1)}, u32[]{:S(2)}) copy-start(bf16[1024,172]{0,1:T(8,128)(2,1)S(1)} %collective-permute-done.7) | copy-start | bytes 1056772
  191.0 12.5 %collective-permute-start.8 = (bf16[1024,172]{0,1:T(8,128)(2,1)S(1)}, bf16[1024,172]{0,1:T(8,128)(2,1)}, u32[]{:S(2)}, u32[]{:S(2)}) collective-permute-start(bf16[1024,172]{0,1:T(8,128)(2,1)S(1)} %collective-permute-done.7), channel_id=1, source_target_pairs={{0,4},{4,8},{8,12},{12,16},{16,20},{20,24},{24,28},{28,0},{1,5},{5... | collective-permute-start | bytes 1056776 | tf_op jit(solution)/shard_map/ppermute | solution.py:14
  203.5 11.7 %collective-permute-start.9 = (bf16[1024,172]{0,1:T(8,128)(2,1)}, bf16[1024,172]{0,1:T(8,128)(2,1)S(1)}, u32[]{:S(2)}, u32[]{:S(2)}) collective-permute-start(bf16[1024,172]{0,1:T(8,128)(2,1)} %collective-permute-done.8), channel_id=1, source_target_pairs={{0,4},{4,8},{8,12},{12,16},{16,20},{20,24},{24,28},{28,0},{1,5},{5... | collective-permute-start | bytes 1056776 | tf_op jit(solution)/shard_map/ppermute | solution.py:14
  208.9 26.1 %all-to-all-start.2 = ((f32[32,24,100]{2,1,0:T(8,128)}), f32[32,24,100]{2,1,0:T(8,128)S(1)}, u32[]{:S(2)}, u32[]{:S(2)}) async-start(f32[32,24,100]{2,1,0:T(8,128)} %bitcast.37), calls=%async_computation.2 | async-start | bytes 786432 | tf_op jit(solution)/shard_map/all_to_all | solution.py:88
  215.2 18.4 %collective-permute-start.10 = (bf16[1024,172]{0,1:T(8,128)(2,1)S(1)}, bf16[1024,172]{0,1:T(8,128)(2,1)S(1)}, u32[]{:S(2)}, u32[]{:S(2)}) collective-permute-start(bf16[1024,172]{0,1:T(8,128)(2,1)S(1)} %collective-permute-done.9), channel_id=1, source_target_pairs={{0,4},{4,8},{8,12},{12,16},{16,20},{20,24},{24,28},{28,0},{1,5},{5... | collective-permute-start | bytes 1056776 | tf_op jit(solution)/shard_map/ppermute | solution.py:14
  233.7 44.0 %collective-permute-start.11 = (bf16[1024,172]{0,1:T(8,128)(2,1)S(1)}, bf16[1024,172]{0,1:T(8,128)(2,1)S(1)}, u32[]{:S(2)}, u32[]{:S(2)}) collective-permute-start(bf16[1024,172]{0,1:T(8,128)(2,1)S(1)} %collective-permute-done.10), channel_id=1, source_target_pairs={{0,4},{4,8},{8,12},{12,16},{16,20},{20,24},{24,28},{28,0},{1,5},{5... | collective-permute-start | bytes 1056776 | tf_op jit(solution)/shard_map/ppermute | solution.py:14
  234.5 70.2 %copy-start.21 = (bf16[1024,172]{0,1:T(8,128)(2,1)S(1)}, bf16[1024,172]{0,1:T(8,128)(2,1)}, u32[]{:S(2)}) copy-start(bf16[1024,172]{0,1:T(8,128)(2,1)} %copy-done.20) | copy-start | bytes 1056772
  277.7 27.1 %copy-start.2 = (f32[768,100]{1,0:T(8,128)}, f32[768,100]{1,0:T(8,128)S(1)}, u32[]{:S(2)}) copy-start(f32[768,100]{1,0:T(8,128)S(1)} %all_gather.14) | copy-start | bytes 921604
  277.7 13.4 %collective-permute-start.12 = (bf16[1024,172]{0,1:T(8,128)(2,1)S(1)}, bf16[1024,172]{0,1:T(8,128)(2,1)S(1)}, u32[]{:S(2)}, u32[]{:S(2)}) collective-permute-start(bf16[1024,172]{0,1:T(8,128)(2,1)S(1)} %collective-permute-done.11), channel_id=1, source_target_pairs={{0,4},{4,8},{8,12},{12,16},{16,20},{20,24},{24,28},{28,0},{1,5},{5... | collective-permute-start | bytes 1056776 | tf_op jit(solution)/shard_map/ppermute | solution.py:14
  291.1 12.5 %collective-permute-start.13 = (bf16[1024,172]{0,1:T(8,128)(2,1)S(1)}, bf16[1024,172]{0,1:T(8,128)(2,1)S(1)}, u32[]{:S(2)}, u32[]{:S(2)}) collective-permute-start(bf16[1024,172]{0,1:T(8,128)(2,1)S(1)} %collective-permute-done.12), channel_id=1, source_target_pairs={{0,4},{4,8},{8,12},{12,16},{16,20},{20,24},{24,28},{28,0},{1,5},{5... | collective-permute-start | bytes 1056776 | tf_op jit(solution)/shard_map/ppermute | solution.py:14
  291.7 33.1 %copy-start.38 = (f32[100]{0:T(128)}, f32[100]{0:T(128)S(1)}, u32[]{:S(2)}) copy-start(f32[100]{0:T(128)S(1)} %get-tuple-element.59) | copy-start | bytes 1204
  310.2 12.4 %copy-start.3 = (f32[768,100]{1,0:T(8,128)S(1)}, f32[768,100]{1,0:T(8,128)}, u32[]{:S(2)}) copy-start(f32[768,100]{1,0:T(8,128)} %copy-done.2) | copy-start | bytes 921604
  310.2 12.4 %copy-start.11 = (f32[172,100]{1,0:T(8,128)S(1)}, f32[172,100]{1,0:T(8,128)}, u32[]{:S(2)}) copy-start(f32[172,100]{1,0:T(8,128)} %param.32) | copy-start | bytes 206404
  322.9 0.9 copy-start.13
  322.9 2.0 copy-start.27
  323.0 2.0 copy-start.35
  323.0 2.0 copy-start.40
  323.1 8.3 %copy-start.32 = (s32[256]{0:T(256)S(1)}, s32[256]{0:T(256)}, u32[]{:S(2)}) copy-start(s32[256]{0:T(256)} %get-tuple-element.64) | copy-start | bytes 3076
  333.3 13.6 %copy-start.41 = (f32[100]{0:T(128)S(1)}, f32[100]{0:T(128)}, u32[]{:S(2)}) copy-start(f32[100]{0:T(128)} %get-tuple-element.31) | copy-start | bytes 1204
  335.2 15.2 %all-to-all-start.1 = ((bf16[8,64,275]{2,1,0:T(8,128)(2,1)}), bf16[8,64,275]{2,1,0:T(8,128)(2,1)}, u32[]{:S(2)}, u32[]{:S(2)}) async-start(bf16[8,64,275]{2,1,0:T(8,128)(2,1)} %bitcast.174), calls=%async_computation.1 | async-start | bytes 786432 | tf_op jit(solution)/shard_map/all_to_all | solution.py:178
  345.1 12.3 %copy-start.16 = (bf16[444,516]{0,1:T(8,128)(2,1)S(1)}, bf16[444,516]{0,1:T(8,128)(2,1)}, u32[]{:S(2)}) copy-start(bf16[444,516]{0,1:T(8,128)(2,1)} %param.28) | copy-start | bytes 1374628
  345.1 14.2 %copy-start.30 = (f32[516]{0:T(1024)S(1)}, f32[516]{0:T(1024)}, u32[]{:S(2)}) copy-start(f32[516]{0:T(1024)} %param.31) | copy-start | bytes 6196
  350.4 19.0 %all-to-all-start.3 = ((f32[32,24,100]{2,1,0:T(8,128)}), f32[32,24,100]{2,1,0:T(8,128)S(1)}, u32[]{:S(2)}, u32[]{:S(2)}) async-start(f32[32,24,100]{2,1,0:T(8,128)} %bitcast.56), calls=%async_computation.3 | async-start | bytes 786432 | tf_op jit(solution)/shard_map/all_to_all | solution.py:88
  356.1 67.2 %all-gather.5.cloned.1.call-start = ((), (), s32[]{:S(2)}) async-start(), calls=%async_computation.5 | async-start | bytes 1966080 | tf_op jit(solution)/shard_map/all_gather | solution.py:179
  357.5 62.1 %copy-start.39 = (f32[100]{0:T(128)S(1)}, f32[100]{0:T(128)}, u32[]{:S(2)}) copy-start(f32[100]{0:T(128)} %copy-done.38) | copy-start | bytes 1204
  423.3 2.1 copy-start.25
  425.4 2.1 copy-start.7
  425.4 2.1 copy-start.17
  425.4 2.1 copy-start.47
  427.5 1.1 copy-start.4
  (4 other events, 2.9 us)
Sparse Core Ops, SparseCore 0:
  152.9 17.4 all-gather.2
  359.4 21.7 all-gather.4
